TPU v7x, 32 devices: a whole 2x2x4 slice. The times are simulated.
32 devices in a mesh: group: 2 (over y), plane: 4 (over z), planey: 2 (over x), ens: 2 (over core).
Axes of the slice: x: 2, y: 2, z: 4, core: 2. Of those that a mesh axis runs over, the one named last changes fastest.
Arguments:
- u_prior: float32 [8, 2, 10, 64, 256], P(('group', 'ens'), None, None, 'plane', 'planey'), parts along dimension 0, may hold values from -6 to 6
- friction_rows: int32 [8], P(('group', 'ens')), parts along dimension 0, may hold values from 0 to 15
- friction_table: float32 [32, 64, 256], P('group', 'plane', 'planey'), parts along dimension 0, may hold values from 0.3 to 3
- bed_fixed: int32 [64, 256], P('plane', 'planey'), may hold values from -536870912 to 536870911
- ice_mask: int32 [64, 256], P('plane', 'planey'), may hold values 0 or 1
Outputs:
- mean_velocity: float32 [4, 10, 64, 256], P('group', None, 'plane', 'planey'), parts along dimension 0
There are 2 independent parts, one for each index of `group`. A program takes and returns all parts, laid end to end along the dimension named above; an argument that names none is the same for every part. Nothing has to cross between parts.
Inputs may be any that keep to these rules, and one draw needn't show every extreme that they name: `friction_rows`: each sample names one row of the friction table.
All inputs are finite; a program needn't handle non-finite values. No bound on the sum of `ice_mask` on one device may be relied on, other than what follows from the above.
Results may differ from a plain program's by a relative error of at most 0.0003.
Values sent between devices are 32-bit elements; how exact they have to be, the bound alone decides.
A program may use at most 64 MiB of HBM per device.

v0:
```python
import jax
import jax.numpy as jnp
from jax import lax
from jax.sharding import PartitionSpec as P

bed_unit = 2.0 ** (-29)
factor_u = (2.0, 1.0, 0.5)
factor_v = (2.0, 0.5, 1.0)


def extended_2(cells, sides, width):
    for axis, dim in sides:
        count = lax.axis_size(axis)
        ends = count - 1
        head = lax.slice_in_dim(cells, 0, width, axis=dim)
        tail = lax.slice_in_dim(cells, cells.shape[dim] - width, cells.shape[dim], axis=dim)
        cells = jnp.concatenate(
            [
                lax.ppermute(tail, axis, [(i, (i + 1) % count) for i in range(ends)]),
                cells,
                lax.ppermute(head, axis, [((i + 1) % count, i) for i in range(ends)]),
            ],
            axis=dim,
        )
    return cells


def coefficient(offset):
    nonzero = len([entry for entry in offset if entry != 0])
    weight_u = 0.25 ** (nonzero - 1)
    weight_v = weight_u
    for dimension in range(3):
        if offset[dimension] != 0:
            weight_u = weight_u * factor_u[dimension]
            weight_v = weight_v * factor_v[dimension]
    return jnp.array([weight_u, weight_v], jnp.float32).reshape(2, 1, 1, 1)


def neighbour_sum(padded):
    layers = padded.shape[-3] - 2
    span_x = padded.shape[-2] - 2
    span_y = padded.shape[-1] - 2
    summed = None
    for step_z in (-1, 0, 1):
        for step_x in (-1, 0, 1):
            for step_y in (-1, 0, 1):
                if step_z == 0 and step_x == 0 and (step_y == 0):
                    continue
                window = padded[
                    ...,
                    1 + step_z : 1 + step_z + layers,
                    1 + step_x : 1 + step_x + span_x,
                    1 + step_y : 1 + step_y + span_y,
                ]
                addend = coefficient((step_z, step_x, step_y)) * window
                summed = addend if summed is None else summed + addend
    return summed


def strain_roots(extended):
    padded = jnp.pad(extended, [(0, 0)] * (extended.ndim - 3) + [(1, 1), (0, 0), (0, 0)])
    along_x = (padded[..., 1:-1, 2:, 1:-1] - padded[..., 1:-1, :-2, 1:-1]) * 0.5
    along_y = (padded[..., 1:-1, 1:-1, 2:] - padded[..., 1:-1, 1:-1, :-2]) * 0.5
    along_z = (padded[..., 2:, 1:-1, 1:-1] - padded[..., :-2, 1:-1, 1:-1]) * 0.5
    stretch_x = along_x[..., 0, :, :, :]
    stretch_y = along_y[..., 1, :, :, :]
    shear_one = along_y[..., 0, :, :, :]
    shear_two = along_x[..., 1, :, :, :]
    vertical_u = along_z[..., 0, :, :, :]
    vertical_v = along_z[..., 1, :, :, :]
    shear = shear_one + shear_two
    strain = (
        stretch_x * stretch_x
        + stretch_y * stretch_y
        + stretch_x * stretch_y
        + 0.25 * shear * shear
        + 0.25 * (vertical_u * vertical_u + vertical_v * vertical_v)
    )
    return jnp.power(strain + 0.1, -1.0 / 6.0)[..., None, :, :, :]


def pad_layers(field):
    return jnp.pad(field, ((0, 0), (0, 0), (1, 1), (0, 0), (0, 0)))


def inner(left, right):
    return jnp.sum(left * right, axis=(1, 2, 3, 4))


def spread(values):
    return values.reshape(-1, 1, 1, 1, 1)


def trimmed(field, margin):
    return field[..., margin:-margin, margin:-margin]


def apply_local(roots_wide, across_part, diag_part, field_wide):
    product = roots_wide * field_wide
    nearby = neighbour_sum(pad_layers(product))
    centre = trimmed(field_wide, 1)
    return trimmed(roots_wide, 1) * (across_part * centre - nearby) + diag_part * centre


def body(u_prior, friction_rows, friction_table, bed_fixed, ice_mask):
    members = u_prior.shape[0]
    layers = u_prior.shape[2]
    rows_x = u_prior.shape[3]
    rows_y = u_prior.shape[4]
    total_x = rows_x * lax.axis_size("plane")
    cover = ice_mask.astype(jnp.float32)
    bed_block = (bed_fixed.astype(jnp.float32) * bed_unit).reshape(1, 1, 1, rows_x, rows_y)
    levels = jnp.arange(friction_table.shape[0], dtype=jnp.int32)
    chosen = (friction_rows[:, None] == levels[None, :]).astype(jnp.float32)
    friction = jnp.sum(chosen[:, :, None, None] * friction_table[None], axis=1)
    bottom = (
        (jnp.arange(layers, dtype=jnp.int32) == 0).astype(jnp.float32).reshape(1, 1, layers, 1, 1)
    )
    mask_block = cover.reshape(1, 1, 1, rows_x, rows_y)
    friction_block = friction.reshape(members, 1, 1, rows_x, rows_y)
    prior_wide, bed_wide, mask_wide, friction_wide = (
        extended_2(u_prior, (("plane", 3), ("planey", 4)), 4),
        extended_2(bed_block, (("plane", 3), ("planey", 4)), 4),
        extended_2(mask_block, (("plane", 3), ("planey", 4)), 4),
        extended_2(friction_block, (("plane", 3), ("planey", 4)), 4),
    )
    roots_three = trimmed(mask_wide, 1) * strain_roots(prior_wide)
    across_two = neighbour_sum(pad_layers(roots_three))
    bed_three = trimmed(bed_wide, 1)
    slope_x = (bed_three[..., 2:, 1:-1] - bed_three[..., :-2, 1:-1]) * 0.5
    slope_y = (bed_three[..., 1:-1, 2:] - bed_three[..., 1:-1, :-2]) * 0.5
    mask_two = trimmed(mask_wide, 2)
    position = (
        lax.axis_index("plane") * rows_x - 2 + jnp.arange(rows_x + 4, dtype=jnp.int32)
    ).astype(jnp.float32)
    thickness = 1.0 + 2.0 * position[:, None] / (total_x - 1)
    force_two = jnp.concatenate(
        [-(mask_two * thickness * slope_x), -(mask_two * thickness * slope_y)], axis=1
    )
    diag_two = mask_two * trimmed(friction_wide, 2) * bottom + (1.0 - mask_two)
    start_three = trimmed(prior_wide, 1) * trimmed(mask_wide, 1)
    residual_two = force_two - apply_local(roots_three, across_two, diag_two, start_three)
    image_one = apply_local(
        trimmed(roots_three, 1), trimmed(across_two, 1), trimmed(diag_two, 1), residual_two
    )
    second_image = apply_local(
        trimmed(roots_three, 2), trimmed(across_two, 2), trimmed(diag_two, 2), image_one
    )
    residual = trimmed(residual_two, 2)
    image = trimmed(image_one, 1)
    gram_rr, gram_ra, gram_aa, gram_ab = lax.psum(
        (
            inner(residual, residual),
            inner(residual, image),
            inner(image, image),
            inner(image, second_image),
        ),
        ("plane", "planey"),
    )
    first_step = gram_rr / gram_ra
    norm_next = gram_rr - 2.0 * first_step * gram_ra + first_step * first_step * gram_aa
    growth = 1.0 + norm_next / gram_rr
    curve = (
        growth * growth * gram_ra
        - 2.0 * growth * first_step * gram_aa
        + first_step * first_step * gram_ab
    )
    second_step = norm_next / curve
    solution = trimmed(start_three, 3)
    solution = (
        solution
        + spread(first_step + second_step * growth) * residual
        - spread(second_step * first_step) * image
    )
    local_sum = jnp.sum(solution, axis=0)
    summed = lax.psum(local_sum, "ens")
    return summed / (members * lax.axis_size("ens"))


def solution(mesh):
    in_specs = (
        P(("group", "ens"), None, None, "plane", "planey"),
        P(("group", "ens")),
        P("group", "plane", "planey"),
        P("plane", "planey"),
        P("plane", "planey"),
    )
    out_specs = P("group", None, "plane", "planey")
    return jax.shard_map(body, mesh=mesh, in_specs=in_specs, out_specs=out_specs, check_vma=False)
```

profile of v0, /device:TPU:0, one launch (start us, length us, event | category | flops | bytes accessed | tf_op | source)
XLA Modules:
  0.0 144.7 jit_solution(11222235841737665456)
XLA Ops:
  6.5 0.7 convert_bitcast_fusion
  7.2 4.9 %collective-permute-start.4 = (f32[1,1,1,4,128]{4,3,2,1,0:T(4,128)S(1)}, f32[1,1,1,4,128]{4,3,2,1,0:T(4,128)S(1)}, u32[]{:S(2)}, u32[]{:S(2)}) collective-permute-start(f32[1,1,1,4,128]{4,3,2,1,0:T(4,128)S(1)} %get-tuple-element.72), channel_id=1, source_target_pairs={{0,4},{4,8},{8,12},{1,5},{5,9},{9,13},{2,6},{6,10},{10,14},{3,7},{... | collective-permute-start | bytes 6152 | tf_op jit(solution)/shard_map/ppermute | solution.py:19
  12.2 1.3 collective-permute-start.5
  13.5 0.7 multiply_bitcast_fusion
  14.2 4.5 %collective-permute-start.8 = (f32[1,1,1,4,128]{4,3,2,1,0:T(4,128)S(1)}, f32[1,1,1,4,128]{4,3,2,1,0:T(4,128)S(1)}, u32[]{:S(2)}, u32[]{:S(2)}) collective-permute-start(f32[1,1,1,4,128]{4,3,2,1,0:T(4,128)S(1)} %get-tuple-element.70), channel_id=1, source_target_pairs={{0,4},{4,8},{8,12},{1,5},{5,9},{9,13},{2,6},{6,10},{10,14},{3,7},{... | collective-permute-start | bytes 6152 | tf_op jit(solution)/shard_map/ppermute | solution.py:19
  18.7 1.3 collective-permute-start.9
  20.0 0.7 compare_convert_fusion.1
  20.8 1.0 multiply_reduce_fusion.3
  21.8 4.5 %collective-permute-start.12 = (f32[2,1,1,4,128]{4,3,0,2,1:T(4,128)S(1)}, f32[2,1,1,4,128]{4,3,0,2,1:T(4,128)S(1)}, u32[]{:S(2)}, u32[]{:S(2)}) collective-permute-start(f32[2,1,1,4,128]{4,3,0,2,1:T(4,128)S(1)} %get-tuple-element.64), channel_id=1, source_target_pairs={{0,4},{4,8},{8,12},{1,5},{5,9},{9,13},{2,6},{6,10},{10,14},{3,7},{... | collective-permute-start | bytes 12296 | tf_op jit(solution)/shard_map/ppermute | solution.py:19
  26.4 1.0 fusion.197
  27.4 1.3 collective-permute-start.13
  28.7 4.6 %collective-permute-start = (f32[2,2,10,4,128]{4,3,2,1,0:T(4,128)S(1)}, f32[2,2,10,4,128]{4,3,2,1,0:T(4,128)S(1)}, u32[]{:S(2)}, u32[]{:S(2)}) collective-permute-start(f32[2,2,10,4,128]{4,3,2,1,0:T(4,128)S(1)} %get-tuple-element.56), channel_id=1, source_target_pairs={{0,4},{4,8},{8,12},{1,5},{5,9},{9,13},{2,6},{6,10},{10,14},{3,7},{... | collective-permute-start | bytes 245768 | tf_op jit(solution)/shard_map/ppermute | solution.py:19
  33.3 0.1 fusion.201
  33.4 3.4 %collective-permute-start.6 = (f32[1,1,1,24,4]{4,3,2,1,0:T(8,128)S(1)}, f32[1,1,1,24,4]{4,3,2,1,0:T(8,128)S(1)}, u32[]{:S(2)}, u32[]{:S(2)}) collective-permute-start(f32[1,1,1,24,4]{4,3,2,1,0:T(8,128)S(1)} %get-tuple-element.68), channel_id=1, source_target_pairs={{0,2},{1,3},{4,6},{5,7},{8,10},{9,11},{12,14},{13,15},{16,18},{17,... | collective-permute-start | bytes 1160 | tf_op jit(solution)/shard_map/ppermute | solution.py:19
  36.8 1.3 collective-permute-start.7
  38.1 0.1 fusion.200
  38.2 4.5 %collective-permute-start.10 = (f32[1,1,1,24,4]{4,3,2,1,0:T(8,128)S(1)}, f32[1,1,1,24,4]{4,3,2,1,0:T(8,128)S(1)}, u32[]{:S(2)}, u32[]{:S(2)}) collective-permute-start(f32[1,1,1,24,4]{4,3,2,1,0:T(8,128)S(1)} %get-tuple-element.66), channel_id=1, source_target_pairs={{0,2},{1,3},{4,6},{5,7},{8,10},{9,11},{12,14},{13,15},{16,18},{17,... | collective-permute-start | bytes 1160 | tf_op jit(solution)/shard_map/ppermute | solution.py:19
  42.7 1.3 collective-permute-start.11
  44.0 0.1 pad_maximum_fusion.6
  44.1 0.0 collective-permute-done.10
  44.1 1.3 collective-permute-start.1
  45.4 2.9 %collective-permute-done.11 = f32[1,1,1,24,4]{4,3,2,1,0:T(8,128)S(1)} collective-permute-done((f32[1,1,1,24,4]{4,3,2,1,0:T(8,128)S(1)}, f32[1,1,1,24,4]{4,3,2,1,0:T(8,128)S(1)}, u32[]{:S(2)}, u32[]{:S(2)}) %collective-permute-start.11) | collective-permute-done | bytes 416 | tf_op jit(solution)/shard_map/ppermute | solution.py:21
  48.3 0.1 pad_maximum_fusion.7
  48.4 0.1 fusion.193
  48.5 0.1 slice_bitcast_fusion.9
  48.6 0.1 fusion.198
  48.7 1.6 %collective-permute-start.14 = (f32[2,1,1,24,4]{4,3,0,2,1:T(8,128)S(1)}, f32[2,1,1,24,4]{4,3,0,2,1:T(8,128)S(1)}, u32[]{:S(2)}, u32[]{:S(2)}) collective-permute-start(f32[2,1,1,24,4]{4,3,0,2,1:T(8,128)S(1)} %get-tuple-element.62), channel_id=1, source_target_pairs={{0,2},{1,3},{4,6},{5,7},{8,10},{9,11},{12,14},{13,15},{16,18},{17,... | collective-permute-start | bytes 2312 | tf_op jit(solution)/shard_map/ppermute | solution.py:19
  50.4 1.3 collective-permute-start.15
  51.7 0.2 collective-permute-done.14
  51.9 4.2 %collective-permute-done.15 = f32[2,1,1,24,4]{4,3,0,2,1:T(8,128)S(1)} collective-permute-done((f32[2,1,1,24,4]{4,3,0,2,1:T(8,128)S(1)}, f32[2,1,1,24,4]{4,3,0,2,1:T(8,128)S(1)}, u32[]{:S(2)}, u32[]{:S(2)}) %collective-permute-start.15) | collective-permute-done | bytes 800 | tf_op jit(solution)/shard_map/ppermute | solution.py:21
  56.1 0.1 fusion.187
  56.2 0.0 copy-start
  56.2 0.1 multiply_add_fusion
  56.3 0.2 slice_bitcast_fusion
  56.5 0.1 multiply_add_fusion.1
  56.7 0.5 copy-done
  57.2 0.1 pad_maximum_fusion.1
  57.2 0.2 fusion.196
  57.4 1.7 %collective-permute-start.2 = (f32[2,2,10,24,4]{4,3,2,1,0:T(8,128)S(1)}, f32[2,2,10,24,4]{4,3,2,1,0:T(8,128)S(1)}, u32[]{:S(2)}, u32[]{:S(2)}) collective-permute-start(f32[2,2,10,24,4]{4,3,2,1,0:T(8,128)S(1)} %get-tuple-element.54), channel_id=1, source_target_pairs={{0,2},{1,3},{4,6},{5,7},{8,10},{9,11},{12,14},{13,15},{16,18},{17,... | collective-permute-start | bytes 46088 | tf_op jit(solution)/shard_map/ppermute | solution.py:19
  59.1 1.3 collective-permute-start.3
  60.4 0.1 slice_bitcast_fusion.7
  60.5 4.9 %collective-permute-done.2 = f32[2,2,10,24,4]{4,3,2,1,0:T(8,128)S(1)} collective-permute-done((f32[2,2,10,24,4]{4,3,2,1,0:T(8,128)S(1)}, f32[2,2,10,24,4]{4,3,2,1,0:T(8,128)S(1)}, u32[]{:S(2)}, u32[]{:S(2)}) %collective-permute-start.2) | collective-permute-done | bytes 15392 | tf_op jit(solution)/shard_map/ppermute | solution.py:19
  65.4 4.4 %collective-permute-done.3 = f32[2,2,10,24,4]{4,3,2,1,0:T(8,128)S(1)} collective-permute-done((f32[2,2,10,24,4]{4,3,2,1,0:T(8,128)S(1)}, f32[2,2,10,24,4]{4,3,2,1,0:T(8,128)S(1)}, u32[]{:S(2)}, u32[]{:S(2)}) %collective-permute-start.3) | collective-permute-done | bytes 15392 | tf_op jit(solution)/shard_map/ppermute | solution.py:21
  69.8 0.6 pad_maximum_fusion
  70.5 1.3 fusion.95
  71.8 0.5 fusion.101
  72.3 5.0 %fusion.103 = (f32[2,10,20,132]{3,2,1,0:T(8,128)S(1)}, f32[2,10,20,132]{3,2,1,0:T(8,128)}, f32[2,10,20,132]{3,2,1,0:T(8,128)}, f32[2,10,20,132]{3,2,1,0:T(8,128)...) fusion(f32[2,1,10,22,134]{4,3,2,1,0:T(8,128)S(1)} %fusion.101), kind=kLoop, calls=%fused_computation.200 | loop fusion | flops 580800 | bytes 4995840 | tf_op jit(solution)/shard_map/mul | solution.py:55
  77.3 2.6 %fusion.133 = (f32[2,10,20,132]{3,2,1,0:T(8,128)}, f32[2,10,20,132]{3,2,1,0:T(8,128)}, f32[2,10,20,132]{3,2,1,0:T(8,128)}, f32[2,10,20,132]{3,2,1,0:T(8,128)}, f...) fusion(f32[2,1,10,22,134]{4,3,2,1,0:T(8,128)S(1)} %fusion.101), kind=kLoop, calls=%fused_computation.240 | loop fusion | flops 158400 | bytes 3379200 | tf_op jit(solution)/shard_map/mul | solution.py:55
  79.9 1.0 slice_bitcast_fusion.1
  80.9 0.8 slice_bitcast_fusion.8
  81.7 0.3 broadcast_multiply_fusion.1
  82.0 0.3 copy-done.2
  82.3 0.0 copy-done.3
  82.3 0.0 copy-done.4
  82.4 0.0 copy-done.5
  82.4 8.9 %broadcast_multiply_fusion.2 = (f32[2,2,10,20,132]{4,3,2,1,0:T(8,128)S(1)}, f32[2,2,10,20,132]{4,3,2,1,0:T(8,128)S(1)}, f32[2,2,10,20,132]{4,3,2,1,0:T(8,128)S(1)}) fusion(f32[2,10,20,132]{3,2,1,0:T(8,128)} %get-tuple-element.53, f32[2,10,20,132]{3,2,1,0:T(8,128)S(1)} %multiply_add_fusion.1, f32[2,2,10,22,134]{4,3,2,1,0:T(8,128)S(1)} %get-tuple-element.21, ...), kind=kLoop, calls=%fused_computation.252 | loop fusion | flops 10032000 | bytes 17623040 | tf_op jit(solution)/shard_map/mul | solution.py:99
  91.3 0.0 copy-start.1
  91.3 5.9 %broadcast_multiply_fusion = (f32[2,2,10,18,130]{4,3,2,1,0:T(8,128)S(1)}, f32[2,2,10,18,130]{4,3,2,1,0:T(8,128)S(1)}) fusion(f32[2,10,18,130]{3,2,1,0:T(8,128)} %slice_bitcast_fusion.1, f32[2,10,18,130]{3,2,1,0:T(8,128)S(1)} %slice_bitcast_fusion, f32[2,2,10,20,132]{4,3,2,1,0:T(8,128)S(1)} %get-tuple-element.18, f32[2]{0:T(128)S(1)} %copy-done.5, ...), kind=kLoop, calls=%fused_computation.249 | loop fusion | flops 5335200 | bytes 12243008 | tf_op jit(solution)/shard_map/mul | solution.py:99
  97.2 1.8 %multiply_reduce_fusion.1 = (f32[2]{0:T(128)S(1)}, f32[2]{0:T(128)S(1)}, f32[2]{0:T(128)S(1)}, f32[2]{0:T(128)S(1)}) fusion(f32[2,2,10,20,132]{4,3,2,1,0:T(8,128)S(1)} %get-tuple-element.19, f32[2,2,10,18,130]{4,3,2,1,0:T(8,128)S(1)} %get-tuple-element.17, f32[2,10,16,128]{3,2,1,0:T(8,128)S(1)} %slice_bitcast_fusion.7, ...), kind=kLoop, calls=%fused_computation.313 | loop fusion | flops 5242872 | bytes 4917280 | tf_op jit(solution)/shard_map/reduce_sum | solution.py:87
  99.0 20.8 %all-reduce.5 = (f32[2]{0:T(128)S(1)}, f32[2]{0:T(128)S(1)}, f32[2]{0:T(128)S(1)}, f32[2]{0:T(128)S(1)}) all-reduce(f32[2]{0:T(128)S(1)} %get-tuple-element.23, f32[2]{0:T(128)S(1)} %get-tuple-element.6, f32[2]{0:T(128)S(1)} %get-tuple-element.7, ...), channel_id=1, replica_groups=mesh['group'=2,'plane'=4,'planey'=2,'ens'=2] {'plane','planey'}, use_global_device_ids=true, to_apply=%region_8.9 | all-reduce | flops 8 | bytes 64 | tf_op jit(solution)/shard_map/psum | solution.py:151
  119.8 1.0 fusion.184
  120.8 0.0 all-reduce.8.cloned.1.call-update
  120.8 15.4 %all-reduce.8.cloned.1.call-done = f32[2,10,16,128]{3,2,1,0:T(8,128)} async-done(((f32[2,10,16,128]{3,2,1,0:T(8,128)}), f32[2,10,16,128]{3,2,1,0:T(8,128)}) %all-reduce.8.cloned.1.call-update) | async-done | bytes 163856 | tf_op jit(solution)/shard_map/psum | solution.py:176
  136.3 1.6 %broadcast_multiply_fusion.3 = f32[2,10,16,128]{3,2,1,0:T(8,128)} fusion(f32[2,10,16,128]{3,2,1,0:T(8,128)} %all-reduce.8.cloned.1.call-done), kind=kLoop, calls=%fused_computation.319 | loop fusion | flops 40960 | bytes 327680 | tf_op jit(solution)/shard_map/div | solution.py:177
  (28 shorter events, 0.1 us)
Async XLA Ops:
  6.5 129.7 %all-reduce.8.cloned.1.call-start = ((), (), s32[]{:S(2)}) async-start(), calls=%async_computation | async-start | bytes 327680 | tf_op jit(solution)/shard_map/psum | solution.py:176
  7.2 20.2 %collective-permute-start.4 = (f32[1,1,1,4,128]{4,3,2,1,0:T(4,128)S(1)}, f32[1,1,1,4,128]{4,3,2,1,0:T(4,128)S(1)}, u32[]{:S(2)}, u32[]{:S(2)}) collective-permute-start(f32[1,1,1,4,128]{4,3,2,1,0:T(4,128)S(1)} %get-tuple-element.72), channel_id=1, source_target_pairs={{0,4},{4,8},{8,12},{1,5},{5,9},{9,13},{2,6},{6,10},{10,14},{3,7},{... | collective-permute-start | bytes 6152 | tf_op jit(solution)/shard_map/ppermute | solution.py:19
  12.2 16.5 %collective-permute-start.5 = (f32[1,1,1,4,128]{4,3,2,1,0:T(4,128)S(1)}, f32[1,1,1,4,128]{4,3,2,1,0:T(4,128)S(1)}, u32[]{:S(2)}, u32[]{:S(2)}) collective-permute-start(f32[1,1,1,4,128]{4,3,2,1,0:T(4,128)S(1)} %get-tuple-element.73), channel_id=1, source_target_pairs={{4,0},{8,4},{12,8},{5,1},{9,5},{13,9},{6,2},{10,6},{14,10},{7,3},{... | collective-permute-start | bytes 6152 | tf_op jit(solution)/shard_map/ppermute | solution.py:21
  14.2 19.2 %collective-permute-start.8 = (f32[1,1,1,4,128]{4,3,2,1,0:T(4,128)S(1)}, f32[1,1,1,4,128]{4,3,2,1,0:T(4,128)S(1)}, u32[]{:S(2)}, u32[]{:S(2)}) collective-permute-start(f32[1,1,1,4,128]{4,3,2,1,0:T(4,128)S(1)} %get-tuple-element.70), channel_id=1, source_target_pairs={{0,4},{4,8},{8,12},{1,5},{5,9},{9,13},{2,6},{6,10},{10,14},{3,7},{... | collective-permute-start | bytes 6152 | tf_op jit(solution)/shard_map/ppermute | solution.py:19
  18.7 18.0 %collective-permute-start.9 = (f32[1,1,1,4,128]{4,3,2,1,0:T(4,128)S(1)}, f32[1,1,1,4,128]{4,3,2,1,0:T(4,128)S(1)}, u32[]{:S(2)}, u32[]{:S(2)}) collective-permute-start(f32[1,1,1,4,128]{4,3,2,1,0:T(4,128)S(1)} %get-tuple-element.71), channel_id=1, source_target_pairs={{4,0},{8,4},{12,8},{5,1},{9,5},{13,9},{6,2},{10,6},{14,10},{7,3},{... | collective-permute-start | bytes 6152 | tf_op jit(solution)/shard_map/ppermute | solution.py:21
  21.8 26.8 %collective-permute-start.12 = (f32[2,1,1,4,128]{4,3,0,2,1:T(4,128)S(1)}, f32[2,1,1,4,128]{4,3,0,2,1:T(4,128)S(1)}, u32[]{:S(2)}, u32[]{:S(2)}) collective-permute-start(f32[2,1,1,4,128]{4,3,0,2,1:T(4,128)S(1)} %get-tuple-element.64), channel_id=1, source_target_pairs={{0,4},{4,8},{8,12},{1,5},{5,9},{9,13},{2,6},{6,10},{10,14},{3,7},{... | collective-permute-start | bytes 12296 | tf_op jit(solution)/shard_map/ppermute | solution.py:19
  27.4 21.2 %collective-permute-start.13 = (f32[2,1,1,4,128]{4,3,0,2,1:T(4,128)S(1)}, f32[2,1,1,4,128]{4,3,0,2,1:T(4,128)S(1)}, u32[]{:S(2)}, u32[]{:S(2)}) collective-permute-start(f32[2,1,1,4,128]{4,3,0,2,1:T(4,128)S(1)} %get-tuple-element.65), channel_id=1, source_target_pairs={{4,0},{8,4},{12,8},{5,1},{9,5},{13,9},{6,2},{10,6},{14,10},{7,3},{... | collective-permute-start | bytes 12296 | tf_op jit(solution)/shard_map/ppermute | solution.py:21
  28.7 27.9 %collective-permute-start = (f32[2,2,10,4,128]{4,3,2,1,0:T(4,128)S(1)}, f32[2,2,10,4,128]{4,3,2,1,0:T(4,128)S(1)}, u32[]{:S(2)}, u32[]{:S(2)}) collective-permute-start(f32[2,2,10,4,128]{4,3,2,1,0:T(4,128)S(1)} %get-tuple-element.56), channel_id=1, source_target_pairs={{0,4},{4,8},{8,12},{1,5},{5,9},{9,13},{2,6},{6,10},{10,14},{3,7},{... | collective-permute-start | bytes 245768 | tf_op jit(solution)/shard_map/ppermute | solution.py:19
  33.4 4.8 %collective-permute-start.6 = (f32[1,1,1,24,4]{4,3,2,1,0:T(8,128)S(1)}, f32[1,1,1,24,4]{4,3,2,1,0:T(8,128)S(1)}, u32[]{:S(2)}, u32[]{:S(2)}) collective-permute-start(f32[1,1,1,24,4]{4,3,2,1,0:T(8,128)S(1)} %get-tuple-element.68), channel_id=1, source_target_pairs={{0,2},{1,3},{4,6},{5,7},{8,10},{9,11},{12,14},{13,15},{16,18},{17,... | collective-permute-start | bytes 1160 | tf_op jit(solution)/shard_map/ppermute | solution.py:19
  36.8 5.9 %collective-permute-start.7 = (f32[1,1,1,24,4]{4,3,2,1,0:T(8,128)S(1)}, f32[1,1,1,24,4]{4,3,2,1,0:T(8,128)S(1)}, u32[]{:S(2)}, u32[]{:S(2)}) collective-permute-start(f32[1,1,1,24,4]{4,3,2,1,0:T(8,128)S(1)} %get-tuple-element.69), channel_id=1, source_target_pairs={{2,0},{3,1},{6,4},{7,5},{10,8},{11,9},{14,12},{15,13},{18,16},{19,... | collective-permute-start | bytes 1160 | tf_op jit(solution)/shard_map/ppermute | solution.py:21
  38.2 5.9 %collective-permute-start.10 = (f32[1,1,1,24,4]{4,3,2,1,0:T(8,128)S(1)}, f32[1,1,1,24,4]{4,3,2,1,0:T(8,128)S(1)}, u32[]{:S(2)}, u32[]{:S(2)}) collective-permute-start(f32[1,1,1,24,4]{4,3,2,1,0:T(8,128)S(1)} %get-tuple-element.66), channel_id=1, source_target_pairs={{0,2},{1,3},{4,6},{5,7},{8,10},{9,11},{12,14},{13,15},{16,18},{17,... | collective-permute-start | bytes 1160 | tf_op jit(solution)/shard_map/ppermute | solution.py:19
  42.7 5.6 %collective-permute-start.11 = (f32[1,1,1,24,4]{4,3,2,1,0:T(8,128)S(1)}, f32[1,1,1,24,4]{4,3,2,1,0:T(8,128)S(1)}, u32[]{:S(2)}, u32[]{:S(2)}) collective-permute-start(f32[1,1,1,24,4]{4,3,2,1,0:T(8,128)S(1)} %get-tuple-element.67), channel_id=1, source_target_pairs={{2,0},{3,1},{6,4},{7,5},{10,8},{11,9},{14,12},{15,13},{18,16},{19,... | collective-permute-start | bytes 1160 | tf_op jit(solution)/shard_map/ppermute | solution.py:21
  44.1 12.5 %collective-permute-start.1 = (f32[2,2,10,4,128]{4,3,2,1,0:T(4,128)S(1)}, f32[2,2,10,4,128]{4,3,2,1,0:T(4,128)S(1)}, u32[]{:S(2)}, u32[]{:S(2)}) collective-permute-start(f32[2,2,10,4,128]{4,3,2,1,0:T(4,128)S(1)} %get-tuple-element.57), channel_id=1, source_target_pairs={{4,0},{8,4},{12,8},{5,1},{9,5},{13,9},{6,2},{10,6},{14,10},{7,3},{... | collective-permute-start | bytes 245768 | tf_op jit(solution)/shard_map/ppermute | solution.py:21
  48.7 3.2 %collective-permute-start.14 = (f32[2,1,1,24,4]{4,3,0,2,1:T(8,128)S(1)}, f32[2,1,1,24,4]{4,3,0,2,1:T(8,128)S(1)}, u32[]{:S(2)}, u32[]{:S(2)}) collective-permute-start(f32[2,1,1,24,4]{4,3,0,2,1:T(8,128)S(1)} %get-tuple-element.62), channel_id=1, source_target_pairs={{0,2},{1,3},{4,6},{5,7},{8,10},{9,11},{12,14},{13,15},{16,18},{17,... | collective-permute-start | bytes 2312 | tf_op jit(solution)/shard_map/ppermute | solution.py:19
  50.4 5.7 %collective-permute-start.15 = (f32[2,1,1,24,4]{4,3,0,2,1:T(8,128)S(1)}, f32[2,1,1,24,4]{4,3,0,2,1:T(8,128)S(1)}, u32[]{:S(2)}, u32[]{:S(2)}) collective-permute-start(f32[2,1,1,24,4]{4,3,0,2,1:T(8,128)S(1)} %get-tuple-element.63), channel_id=1, source_target_pairs={{2,0},{3,1},{6,4},{7,5},{10,8},{11,9},{14,12},{15,13},{18,16},{19,... | collective-permute-start | bytes 2312 | tf_op jit(solution)/shard_map/ppermute | solution.py:21
  56.2 1.0 copy-start
  57.4 8.0 %collective-permute-start.2 = (f32[2,2,10,24,4]{4,3,2,1,0:T(8,128)S(1)}, f32[2,2,10,24,4]{4,3,2,1,0:T(8,128)S(1)}, u32[]{:S(2)}, u32[]{:S(2)}) collective-permute-start(f32[2,2,10,24,4]{4,3,2,1,0:T(8,128)S(1)} %get-tuple-element.54), channel_id=1, source_target_pairs={{0,2},{1,3},{4,6},{5,7},{8,10},{9,11},{12,14},{13,15},{16,18},{17,... | collective-permute-start | bytes 46088 | tf_op jit(solution)/shard_map/ppermute | solution.py:19
  59.1 10.7 %collective-permute-start.3 = (f32[2,2,10,24,4]{4,3,2,1,0:T(8,128)S(1)}, f32[2,2,10,24,4]{4,3,2,1,0:T(8,128)S(1)}, u32[]{:S(2)}, u32[]{:S(2)}) collective-permute-start(f32[2,2,10,24,4]{4,3,2,1,0:T(8,128)S(1)} %get-tuple-element.55), channel_id=1, source_target_pairs={{2,0},{3,1},{6,4},{7,5},{10,8},{11,9},{14,12},{15,13},{18,16},{19,... | collective-permute-start | bytes 46088 | tf_op jit(solution)/shard_map/ppermute | solution.py:21
  81.7 0.7 copy-start.2
  81.7 0.7 copy-start.3
  81.7 0.7 copy-start.4
  81.7 0.7 copy-start.5
  91.3 5.9 %copy-start.1 = (f32[2,10,16,128]{3,2,1,0:T(8,128)S(1)}, f32[2,10,16,128]{3,2,1,0:T(8,128)}, u32[]{:S(2)}) copy-start(f32[2,10,16,128]{3,2,1,0:T(8,128)} %slice_bitcast_fusion.8) | copy-start | bytes 491524
Sparse Core Ops, SparseCore 0:
  120.9 15.2 all-reduce.7
where the time goes:
time: 146 us; the launch traced here: 145 us
  starting transfers between devices  40.1 us (27%)
  other arithmetic  33.4 us (23%)
  waiting for transfers between devices  32.1 us (22%)
  blocking collectives  20.8 us (14%)
  between operations  13.8 us (9%)
  local copies, waits for them, and re-layouts  4.52 us (3%)
    ppermute x8, starting transfers between devices, extended_2(): lax.ppermute(tail, axis, [(i, (i + 1) % count) for i in range(ends)])  29.8 us
    psum x1, blocking collectives, body(): lax.psum((inner(residual, residual), inner(residual, image), inner(image,...  20.8 us
    psum x1, waiting for transfers between devices, body(): summed = lax.psum(local_sum, 'ens')  15.4 us
    mul x3, other arithmetic, apply_local(): product = roots_wide * field_wide  15.1 us
    ppermute x8, waiting for transfers between devices, extended_2(): lax.ppermute(head, axis, [((i + 1) % count, i) for i in range(ends)])  11.6 us
    ppermute x8, starting transfers between devices, extended_2(): lax.ppermute(head, axis, [((i + 1) % count, i) for i in range(ends)])  10.3 us
    mul x2, other arithmetic, neighbour_sum(): addend = coefficient((step_z, step_x, step_y)) * window  7.6 us
    ppermute x8, waiting for transfers between devices, extended_2(): lax.ppermute(tail, axis, [(i, (i + 1) % count) for i in range(ends)])  5.09 us
  transfers between devices with their start and end apart: 17, of which 6 were waited for; matrix products, arithmetic and copies ran while one was open for 3% of the time, Pallas kernels for 0%

commit v1 on v0

v1 whole, which is shorter than its diff:
```python
import functools
import jax
import jax.numpy as jnp
from jax import lax
from jax.experimental import pallas as pl
from jax.experimental.pallas import tpu as pltpu
from jax.sharding import PartitionSpec as P

bed_unit = 2.0 ** (-29)
HALO = 4
SLOTS = 16
STEP_I = (0.25, 0.125)
STEP_J = (0.125, 0.25)


def iota(shape, dim):
    return lax.broadcasted_iota(jnp.int32, shape, dim)


def shift_i(x, step):
    return pltpu.roll(x, (-step) % x.shape[-2], x.ndim - 2)


def shift_j(x, step):
    rolled = pltpu.roll(x, (-step) % x.shape[-1], x.ndim - 1)
    swapped = jnp.concatenate([rolled[1:2], rolled[0:1]], axis=0)
    lane = iota(x.shape, x.ndim - 1)
    edge = 0 if step < 0 else x.shape[-1] - 1
    return jnp.where(lane == edge, swapped, rolled)


def spread_ij(x, c):
    x = x + STEP_I[c] * (shift_i(x, 1) + shift_i(x, -1))
    return x + STEP_J[c] * (shift_j(x, 1) + shift_j(x, -1))


def spread_z(ref, index, z):
    return ref[index + (z + 1,)] + 0.5 * (ref[index + (z,)] + ref[index + (z + 2,)])


def kernel(sizes, rows_ref, u_hbm, table_hbm, bed_hbm, mask_hbm, out_ref,
           u_v, table_v, bed_v, mask_v,
           up_s, down_s, side_s, corner_s,
           below_r, above_r, side_r, corner_r, hx,
           ext, roots, tr, pa, pb, r_ext, a_ext, force,
           r_core, a_core, w_core, r_peer, a_peer, w_peer,
           gram_s, gram_r,
           in_sem, halo_send, halo_recv, peer_send, peer_recv, gram_send, gram_recv):
    np_, nq, ne = sizes
    members, _, layers, rows, cols = u_v.shape
    ring = rows + 2 * HALO
    ix, iy, ie = lax.axis_index("plane"), lax.axis_index("planey"), lax.axis_index("ens")

    loads = [
        pltpu.make_async_copy(src, dst, in_sem.at[i])
        for i, (src, dst) in enumerate(
            ((u_hbm, u_v), (table_hbm, table_v), (bed_hbm, bed_v), (mask_hbm, mask_v))
        )
    ]
    for load in loads:
        load.start()

    def group_target(d):
        de, rest = d // (np_ * nq), d % (np_ * nq)
        return {
            "plane": lax.rem(ix + rest // nq, np_),
            "planey": lax.rem(iy + rest % nq, nq),
            "ens": lax.rem(ie + de, ne),
        }

    total = np_ * nq * ne

    def each_peer(fn):
        if total <= 32:
            for d in range(1, total):
                fn(d)
        else:
            def step(d, carry):
                fn(d)
                return carry
            lax.fori_loop(1, total, step, 0)

    barrier = pltpu.get_barrier_semaphore()
    each_peer(lambda d: pl.semaphore_signal(
        barrier, inc=1, device_id=group_target(d), device_id_type=pl.DeviceIdType.MESH))

    flows = []
    for i, (dx, dy, src, dst) in enumerate((
        (-1, 0, up_s, below_r),
        (1, 0, down_s, above_r),
        (0, -1, side_s, side_r.at[1]),
        (0, 1, side_s, side_r.at[0]),
        (-1, -1, corner_s, corner_r.at[0, 1]),
        (-1, 1, corner_s, corner_r.at[0, 0]),
        (1, -1, corner_s, corner_r.at[1, 1]),
        (1, 1, corner_s, corner_r.at[1, 0]),
    )):
        tx, ty = ix + dx, iy + dy
        sx, sy = ix - dx, iy - dy
        to_ok = (tx >= 0) & (tx < np_) & (ty >= 0) & (ty < nq)
        from_ok = (sx >= 0) & (sx < np_) & (sy >= 0) & (sy < nq)
        copy = pltpu.make_async_remote_copy(
            src_ref=src, dst_ref=dst, send_sem=halo_send.at[i], recv_sem=halo_recv.at[i],
            device_id={"plane": jnp.clip(tx, 0, np_ - 1), "planey": jnp.clip(ty, 0, nq - 1)},
            device_id_type=pl.DeviceIdType.MESH)
        flows.append((copy, to_ok, from_ok, dst))

    for load in loads:
        load.wait()

    planes = [(lambda m=m, c=c, z=z: u_v[m, c, z])
              for m in range(members) for z in range(layers) for c in range(2)]
    first_extra = len(planes)
    planes.append(lambda: bed_v[...].astype(jnp.float32) * bed_unit)
    planes.append(lambda: mask_v[...].astype(jnp.float32))
    for m in range(members):
        planes.append(lambda m=m: table_v[rows_ref[m]])
    if len(planes) % 2:
        planes.append(planes[-1])
    groups = side_s.shape[0]

    low8 = iota((8, cols), 0) < 4
    lane_x = iota((rows, cols), 1)
    for g in range(groups):
        packed = jnp.zeros((rows, cols), jnp.float32)
        for k in range(SLOTS):
            p = g * SLOTS + k
            if p >= len(planes):
                continue
            rolled = pltpu.roll(planes[p](), (8 * k + 4) % cols, 1)
            packed = jnp.where((lane_x // 8) == k, rolled, packed)
        side_s[g] = packed
        corner_s[g] = jnp.where(low8, packed[0:8], packed[rows - 8:rows])

    def ends(value):
        return jnp.where(low8, value[0:8], value[rows - 8:rows])

    for i in range(len(planes) // 2):
        first = ends(planes[2 * i]())
        turned = pltpu.roll(ends(planes[2 * i + 1]()), 4, 0)
        up_s[i] = jnp.where(low8, first, turned)
        down_s[i] = jnp.where(low8, turned, first)

    pl.semaphore_wait(barrier, total - 1)
    for copy, to_ok, from_ok, dst in flows:
        pl.when(to_ok)(copy.start)

    for copy, to_ok, from_ok, dst in flows:
        @pl.when(jnp.logical_not(from_ok))
        def _(dst=dst):
            dst[...] = jnp.zeros(dst.shape, jnp.float32)
    zero = jnp.zeros((2, ring, cols), jnp.float32)
    for m in range(members):
        for end in (0, layers + 1):
            roots[m, end] = zero
            for c in range(2):
                ext[m, c, end] = zero
                pa[m, c, end] = zero
                pb[m, c, end] = zero
    cover_core = mask_v[...].astype(jnp.float32)
    for c in range(2):
        for z in range(layers):
            summed = u_v[0, c, z]
            for m in range(1, members):
                summed = summed + u_v[m, c, z]
            w_core[c, z] = cover_core * summed

    for copy, to_ok, from_ok, dst in flows:
        pl.when(from_ok)(copy.wait_recv)

    lane_h = iota((rows, cols), 1)
    lane_8 = iota((8, cols), 1)
    for g in range(groups):
        hx[g, 0:rows] = jnp.where(lane_h % 8 < 4, side_r[0, g], side_r[1, g])
        left = jnp.where(low8, corner_r[0, 0, g], corner_r[1, 0, g])
        right = jnp.where(low8, corner_r[0, 1, g], corner_r[1, 1, g])
        hx[g, rows:ring] = jnp.where(lane_8 % 8 < 4, left, right)

    def tail(p):
        i = p // 2
        if p % 2 == 0:
            return jnp.where(low8, below_r[i], above_r[i])
        return pltpu.roll(jnp.where(low8, above_r[i], below_r[i]), 4, 0)

    def extended(p):
        core = jnp.concatenate([planes[p](), tail(p)], axis=0)
        k = p % SLOTS
        halo = pltpu.roll(hx[p // SLOTS], (-(8 * k + 4)) % cols, 1)
        return jnp.stack([core, halo])

    p = 0
    for m in range(members):
        for z in range(layers):
            for c in range(2):
                ext[m, c, z + 1] = extended(p)
                p += 1
    bed = extended(first_extra)
    cover = extended(first_extra + 1)
    row = iota((2, ring, cols), 1)
    position = (ix * rows + jnp.where(row < rows + HALO, row, row - ring)).astype(jnp.float32)
    thickness = 1.0 + 2.0 * position / (np_ * rows - 1)
    slope_x = (shift_i(bed, 1) - shift_i(bed, -1)) * 0.5
    slope_y = (shift_j(bed, 1) - shift_j(bed, -1)) * 0.5
    force[0] = -(cover * thickness * slope_x)
    force[1] = -(cover * thickness * slope_y)
    force[2] = cover
    for m in range(members):
        force[3 + m] = cover * extended(first_extra + 2 + m)

    def roots_step(z, carry):
        cover = force[2]
        for m in range(members):
            u, v = ext[m, 0, z + 1], ext[m, 1, z + 1]
            u_i = (shift_i(u, 1) - shift_i(u, -1)) * 0.5
            v_j = (shift_j(v, 1) - shift_j(v, -1)) * 0.5
            shear = ((shift_j(u, 1) - shift_j(u, -1)) + (shift_i(v, 1) - shift_i(v, -1))) * 0.5
            u_z = (ext[m, 0, z + 2] - ext[m, 0, z]) * 0.5
            v_z = (ext[m, 1, z + 2] - ext[m, 1, z]) * 0.5
            strain = (u_i * u_i + v_j * v_j + u_i * v_j + 0.25 * shear * shear
                      + 0.25 * (u_z * u_z + v_z * v_z))
            root = cover * jnp.exp(jnp.log(strain + 0.1) * (-1.0 / 6.0))
            roots[m, z + 1] = root
            pa[m, 0, z + 1] = root * u
            pa[m, 1, z + 1] = root * v
        return carry

    lax.fori_loop(0, layers, roots_step, 0)

    def image(m, c, z, field, p_ref):
        across = tr[m, c, z]
        bottom = jnp.where(z == 0, 1.0, 0.0).astype(jnp.float32)
        diag = force[3 + m] * bottom + (1.0 - force[2])
        spread = spread_ij(spread_z(p_ref, (m, c), z), c)
        return 4.0 * roots[m, z + 1] * (across * field - spread) + diag * field

    zero_core = jnp.zeros((rows, cols), jnp.float32)

    def residual_step(z, carry):
        carry = list(carry)
        for m in range(members):
            near = spread_z(roots, (m,), z)
            for c in range(2):
                tr[m, c, z] = spread_ij(near, c)
                start = force[2] * ext[m, c, z + 1]
                r = force[c] - image(m, c, z, start, pa)
                r_ext[m, c, z] = r
                pb[m, c, z + 1] = roots[m, z + 1] * r
                core = r[0, 0:rows]
                r_core[m, c, z] = core
                carry[m] = carry[m] + core * core
        return tuple(carry)

    rr = lax.fori_loop(0, layers, residual_step, (zero_core,) * members)

    peer = {"ens": lax.rem(ie + 1, ne)}

    def to_peer(i, src, dst):
        return pltpu.make_async_remote_copy(
            src_ref=src, dst_ref=dst, send_sem=peer_send.at[i], recv_sem=peer_recv.at[i],
            device_id=peer, device_id_type=pl.DeviceIdType.MESH)

    peer_flows = [to_peer(0, w_core, w_peer), to_peer(1, r_core, r_peer), to_peer(2, a_core, a_peer)]
    peer_flows[0].start()

    def image_step(z, carry):
        carry = list(carry)
        for m in range(members):
            for c in range(2):
                r = r_ext[m, c, z]
                a = image(m, c, z, r, pb)
                a_ext[m, c, z] = a
                pa[m, c, z + 1] = roots[m, z + 1] * a
                core = a[0, 0:rows]
                a_core[m, c, z] = core
                carry[2 * m] = carry[2 * m] + r[0, 0:rows] * core
                carry[2 * m + 1] = carry[2 * m + 1] + core * core
        return tuple(carry)

    ra_aa = lax.fori_loop(0, layers, image_step, (zero_core,) * (2 * members))
    peer_flows[1].start()

    def second_step(z, carry):
        carry = list(carry)
        for m in range(members):
            for c in range(2):
                a = a_ext[m, c, z]
                b = image(m, c, z, a, pa)
                carry[m] = carry[m] + a[0, 0:rows] * b[0, 0:rows]
        return tuple(carry)

    ab = lax.fori_loop(0, layers, second_step, (zero_core,) * members)
    peer_flows[2].start()

    lane_1 = iota((1, cols), 1)
    mine = jnp.zeros((1, cols), jnp.float32)
    for m in range(members):
        for q, acc in enumerate((rr[m], ra_aa[2 * m], ra_aa[2 * m + 1], ab[m])):
            value = jnp.sum(jnp.sum(acc, axis=0, keepdims=True), axis=1, keepdims=True)
            mine = jnp.where(lane_1 == 4 * m + q, value, mine)
    gram_s[0] = mine

    def gram_copy(d):
        return pltpu.make_async_remote_copy(
            src_ref=gram_s, dst_ref=gram_r.at[pl.ds(d, 1)],
            send_sem=gram_send, recv_sem=gram_recv,
            device_id=group_target(d), device_id_type=pl.DeviceIdType.MESH)

    each_peer(lambda d: gram_copy(d).start())
    everything = pltpu.make_async_remote_copy(
        src_ref=gram_r.at[pl.ds(1, total - 1)], dst_ref=gram_r.at[pl.ds(1, total - 1)],
        send_sem=gram_send, recv_sem=gram_recv,
        device_id=group_target(1), device_id_type=pl.DeviceIdType.MESH)
    everything.wait_recv()

    half = np_ * nq
    own = mine
    if half > 1:
        own = own + jnp.sum(gram_r[1:half], axis=0)
    sums = [own] + [jnp.sum(gram_r[half * e:half * (e + 1)], axis=0) for e in range(1, ne)]
    steps = []
    for e in range(ne):
        for m in range(members):
            g_rr, g_ra, g_aa, g_ab = [
                jnp.sum(jnp.where(lane_1 == 4 * m + q, sums[e], 0.0), axis=1, keepdims=True)
                for q in range(4)
            ]
            first = g_rr / g_ra
            following = g_rr - 2.0 * first * g_ra + first * first * g_aa
            growth = 1.0 + following / g_rr
            curve = (growth * growth * g_ra - 2.0 * growth * first * g_aa
                     + first * first * g_ab)
            second = following / curve
            share = 1.0 / (members * ne)
            steps.append(((first + second * growth) * share, second * first * share))

    for flow in peer_flows:
        flow.wait_recv()
    share = 1.0 / (members * ne)

    def final_step(z, carry):
        for c in range(2):
            value = share * (w_core[c, z] + w_peer[c, z])
            for m in range(members):
                value = value + steps[m][0] * r_core[m, c, z] - steps[m][1] * a_core[m, c, z]
                one, two = steps[members + m]
                value = value + one * r_peer[m, c, z] - two * a_peer[m, c, z]
            out_ref[c, z] = value
        return carry

    lax.fori_loop(0, layers, final_step, 0)

    for copy, to_ok, from_ok, dst in flows:
        pl.when(to_ok)(copy.wait_send)
    for flow in peer_flows:
        flow.wait_send()
    everything.wait_send()


def body(sizes, u_prior, friction_rows, friction_table, bed_fixed, ice_mask):
    members, _, layers, rows, cols = u_prior.shape
    levels = friction_table.shape[0]
    total = sizes[0] * sizes[1] * sizes[2]
    ring = rows + 2 * HALO
    planes = members * layers * 2 + 2 + members
    pairs = (planes + 1) // 2
    groups = (2 * pairs + SLOTS - 1) // SLOTS
    f32 = jnp.float32
    any_space = pl.BlockSpec(memory_space=pl.ANY)
    vmem = lambda *shape: pltpu.VMEM(shape, f32)
    core = (members, 2, layers, rows, cols)
    wide = (2, ring, cols)
    return pl.pallas_call(
        functools.partial(kernel, sizes),
        out_shape=jax.ShapeDtypeStruct((2, layers, rows, cols), f32),
        in_specs=[pl.BlockSpec(memory_space=pltpu.SMEM)] + [any_space] * 4,
        out_specs=pl.BlockSpec(memory_space=pltpu.VMEM),
        scratch_shapes=[
            vmem(*core), vmem(levels, rows, cols),
            pltpu.VMEM((rows, cols), jnp.int32), pltpu.VMEM((rows, cols), jnp.int32),
            vmem(pairs, 8, cols), vmem(pairs, 8, cols), vmem(groups, rows, cols), vmem(groups, 8, cols),
            vmem(pairs, 8, cols), vmem(pairs, 8, cols), vmem(2, groups, rows, cols),
            vmem(2, 2, groups, 8, cols), vmem(groups, ring, cols),
            vmem(members, 2, layers + 2, *wide), vmem(members, layers + 2, *wide),
            vmem(members, 2, layers, *wide),
            vmem(members, 2, layers + 2, *wide), vmem(members, 2, layers + 2, *wide),
            vmem(members, 2, layers, *wide), vmem(members, 2, layers, *wide),
            vmem(3 + members, *wide),
            vmem(*core), vmem(*core), vmem(*core[1:]),
            vmem(*core), vmem(*core), vmem(*core[1:]),
            vmem(1, 1, cols), vmem(total, 1, cols),
            pltpu.SemaphoreType.DMA((4,)),
            pltpu.SemaphoreType.DMA((8,)), pltpu.SemaphoreType.DMA((8,)),
            pltpu.SemaphoreType.DMA((3,)), pltpu.SemaphoreType.DMA((3,)),
            pltpu.SemaphoreType.DMA, pltpu.SemaphoreType.DMA,
        ],
        compiler_params=pltpu.CompilerParams(
            collective_id=0, has_side_effects=True, vmem_limit_bytes=40 * 1024 * 1024),
        name="picard",
    )(friction_rows, u_prior, friction_table, bed_fixed, ice_mask)


def solution(mesh):
    sizes = (mesh.shape["plane"], mesh.shape["planey"], mesh.shape["ens"])
    in_specs = (
        P(("group", "ens"), None, None, "plane", "planey"),
        P(("group", "ens")),
        P("group", "plane", "planey"),
        P("plane", "planey"),
        P("plane", "planey"),
    )
    out_specs = P("group", None, "plane", "planey")
    return jax.shard_map(functools.partial(body, sizes), mesh=mesh, in_specs=in_specs,
                         out_specs=out_specs, check_vma=False)
```

time: 146 us -> 26.5 us (0.18)
  starting transfers between devices: 40.1 us -> 0 us
  other arithmetic: 33.4 us -> 0 us
  waiting for transfers between devices: 32.1 us -> 0 us
  Pallas kernels: 0 us -> 21.6 us
  blocking collectives: 20.8 us -> 0 us
  between operations: 13.8 us -> 0.01 us
    ppermute x16 -> x0, starting transfers between devices: 40.1 us -> none  [the longest x8 29.8 us: extended_2(): lax.ppermute(tail, axis, [(i, (i + 1) % count) for i in range(ends)])]
    mul x9 -> x0, other arithmetic: 24.6 us -> none  [the longest x3 15.1 us: apply_local(): product = roots_wide * field_wide]
    pallas_call x0 -> x1, Pallas kernels: none -> 21.6 us  [body(): pl.pallas_call(functools.partial(kernel, sizes), out_shape=jax.ShapeDtype...]
    psum x1 -> x0, blocking collectives: 20.8 us -> none  [body(): lax.psum((inner(residual, residual), inner(residual, image), inner(image,...]
    ppermute x16 -> x0, waiting for transfers between devices: 16.6 us -> none  [the longest x8 11.6 us: extended_2(): lax.ppermute(head, axis, [((i + 1) % count, i) for i in range(ends)])]
    psum x1 -> x0, waiting for transfers between devices: 15.4 us -> none  [body(): summed = lax.psum(local_sum, 'ens')]
    reduce_sum x3 -> x0, other arithmetic: 3.79 us -> none  [the longest x1 1.79 us: inner(): return jnp.sum(left * right, axis=(1, 2, 3, 4))]
    unnamed x12 -> x11, local copies, waits for them, and re-layouts: 0.87 us -> 4.59 us
  transfers between devices with their start and end apart: 17 -> 0, of which waited for: 6 -> 0; matrix products, arithmetic and copies ran while one was open for 3% -> 0% of each run, Pallas kernels for 0% -> 0%
where the time goes in v1:
time: 26.5 us; the launch traced here: 26.2 us
  Pallas kernels  21.6 us (82%)
  local copies, waits for them, and re-layouts  4.59 us (17%)
    pallas_call x1, Pallas kernels, body(): pl.pallas_call(functools.partial(kernel, sizes), out_shape=jax.ShapeDtype...  21.6 us
    unnamed x11, local copies, waits for them, and re-layouts  4.59 us

profile of v1, /device:TPU:0, one launch (start us, length us, event | category | flops | bytes accessed | tf_op | source)
XLA Modules:
  0.0 26.2 jit_solution(17542269854581304306)
XLA Ops:
  0.0 0.0 copy-start
  0.0 1.0 %copy-done = f32[2,2,10,16,128]{4,3,2,1,0:T(8,128)S(1)} copy-done((f32[2,2,10,16,128]{4,3,2,1,0:T(8,128)S(1)}, f32[2,2,10,16,128]{4,3,2,1,0:T(8,128)}, u32[]{:S(2)}) %copy-start) | copy-done | bytes 327704
  1.0 0.0 copy-start.1
  1.0 0.9 %copy-done.1 = f32[16,16,128]{2,1,0:T(8,128)S(1)} copy-done((f32[16,16,128]{2,1,0:T(8,128)S(1)}, f32[16,16,128]{2,1,0:T(8,128)}, u32[]{:S(2)}) %copy-start.1) | copy-done | bytes 131096
  1.9 0.0 copy-start.2
  1.9 0.7 %copy-done.2 = s32[16,128]{1,0:T(8,128)S(1)} copy-done((s32[16,128]{1,0:T(8,128)S(1)}, s32[16,128]{1,0:T(8,128)}, u32[]{:S(2)}) %copy-start.2) | copy-done | bytes 8216
  2.6 0.0 copy-start.3
  2.6 0.7 %copy-done.3 = s32[16,128]{1,0:T(8,128)S(1)} copy-done((s32[16,128]{1,0:T(8,128)S(1)}, s32[16,128]{1,0:T(8,128)}, u32[]{:S(2)}) %copy-start.3) | copy-done | bytes 8216
  3.3 0.0 copy-start.4
  3.3 0.7 %copy-done.4 = s32[2]{0:T(128)S(1)} copy-done((s32[2]{0:T(128)S(1)}, s32[2]{0:T(128)}, u32[]{:S(2)}) %copy-start.4) | copy-done | bytes 32
  3.9 21.6 %picard.1 = f32[2,10,16,128]{3,2,1,0:T(8,128)S(1)} custom-call(s32[2]{0:T(128)S(1)} %copy-done.4, f32[2,2,10,16,128]{4,3,2,1,0:T(8,128)S(1)} %copy-done, f32[16,16,128]{2,1,0:T(8,128)S(1)} %copy-done.1, s32[16,128]{1,0:T(8,128)S(1)} %copy-done.2, s32[16,128]{1,0:T(8,128)S(1)} %copy-done.3), custom_call_target="tpu_custom_call" | custom-call | tf_op jit(solution)/shard_map/picard/pallas_call | solution.py:372
  25.5 0.7 %copy.7 = f32[2,10,16,128]{3,2,1,0:T(8,128)} copy(f32[2,10,16,128]{3,2,1,0:T(8,128)S(1)} %picard.1) | data formatting | bytes 327680
Async XLA Ops:
  0.0 1.0 %copy-start = (f32[2,2,10,16,128]{4,3,2,1,0:T(8,128)S(1)}, f32[2,2,10,16,128]{4,3,2,1,0:T(8,128)}, u32[]{:S(2)}) copy-start(f32[2,2,10,16,128]{4,3,2,1,0:T(8,128)} %u_hbm.1) | copy-start | bytes 983044
  1.0 0.9 %copy-start.1 = (f32[16,16,128]{2,1,0:T(8,128)S(1)}, f32[16,16,128]{2,1,0:T(8,128)}, u32[]{:S(2)}) copy-start(f32[16,16,128]{2,1,0:T(8,128)} %table_hbm.1) | copy-start | bytes 393220
  1.9 0.7 %copy-start.2 = (s32[16,128]{1,0:T(8,128)S(1)}, s32[16,128]{1,0:T(8,128)}, u32[]{:S(2)}) copy-start(s32[16,128]{1,0:T(8,128)} %bed_hbm.1) | copy-start | bytes 24580
  2.6 0.7 %copy-start.3 = (s32[16,128]{1,0:T(8,128)S(1)}, s32[16,128]{1,0:T(8,128)}, u32[]{:S(2)}) copy-start(s32[16,128]{1,0:T(8,128)} %mask_hbm.1) | copy-start | bytes 24580
  3.3 0.7 %copy-start.4 = (s32[2]{0:T(128)S(1)}, s32[2]{0:T(128)}, u32[]{:S(2)}) copy-start(s32[2]{0:T(128)} %rows_ref.1) | copy-start | bytes 28

commit v2 on v1

--- a/solution.py
+++ b/solution.py
@@ -38,23 +38,52 @@
     return ref[index + (z + 1,)] + 0.5 * (ref[index + (z,)] + ref[index + (z + 2,)])
 
 
-def kernel(sizes, rows_ref, u_hbm, table_hbm, bed_hbm, mask_hbm, out_ref,
-           u_v, table_v, bed_v, mask_v,
+def kernel(sizes, rows_hbm, u_hbm, table_hbm, bed_hbm, mask_hbm, out_ref,
+           rows_ref, u_v, table_v, bed_v, mask_v,
            up_s, down_s, side_s, corner_s,
            below_r, above_r, side_r, corner_r, hx,
            ext, roots, tr, pa, pb, r_ext, a_ext, force,
            r_core, a_core, w_core, r_peer, a_peer, w_peer,
            gram_s, gram_r,
-           in_sem, halo_send, halo_recv, peer_send, peer_recv, gram_send, gram_recv):
+           relay, in_sem, halo_send, halo_recv, peer_send, peer_recv, gram_send, gram_recv):
     np_, nq, ne = sizes
     members, _, layers, rows, cols = u_v.shape
     ring = rows + 2 * HALO
     ix, iy, ie = lax.axis_index("plane"), lax.axis_index("planey"), lax.axis_index("ens")
 
+    total = np_ * nq * ne
+    mesh_id = pl.DeviceIdType.MESH
+
+    adjacent = []
+    for dx in (0, -1, 1):
+        for dy in (0, -1, 1):
+            for de in range(ne):
+                if (dx, dy, de) == (0, 0, 0):
+                    continue
+                tx, ty = ix + dx, iy + dy
+                ok = (tx >= 0) & (tx < np_) & (ty >= 0) & (ty < nq)
+                where = {"plane": jnp.clip(tx, 0, np_ - 1), "planey": jnp.clip(ty, 0, nq - 1),
+                         "ens": lax.rem(ie + de, ne)}
+                adjacent.append((ok, where))
+    span_x = 1 + (ix > 0).astype(jnp.int32) + (ix < np_ - 1).astype(jnp.int32)
+    span_y = 1 + (iy > 0).astype(jnp.int32) + (iy < nq - 1).astype(jnp.int32)
+    adjacent_count = span_x * span_y * ne - 1
+    rounds = max(max(np_, nq) - 2, 0)
+
+    def signal_adjacent(sem):
+        for ok, where in adjacent:
+            @pl.when(ok)
+            def _(where=where):
+                pl.semaphore_signal(sem, inc=1, device_id=where, device_id_type=mesh_id)
+
+    barrier = pltpu.get_barrier_semaphore()
+    signal_adjacent(barrier)
+
     loads = [
         pltpu.make_async_copy(src, dst, in_sem.at[i])
         for i, (src, dst) in enumerate(
-            ((u_hbm, u_v), (table_hbm, table_v), (bed_hbm, bed_v), (mask_hbm, mask_v))
+            ((u_hbm, u_v), (table_hbm, table_v), (bed_hbm, bed_v), (mask_hbm, mask_v),
+             (rows_hbm, rows_ref))
         )
     ]
     for load in loads:
@@ -67,8 +96,6 @@
             "planey": lax.rem(iy + rest % nq, nq),
             "ens": lax.rem(ie + de, ne),
         }
-
-    total = np_ * nq * ne
 
     def each_peer(fn):
         if total <= 32:
@@ -79,10 +106,6 @@
                 fn(d)
                 return carry
             lax.fori_loop(1, total, step, 0)
-
-    barrier = pltpu.get_barrier_semaphore()
-    each_peer(lambda d: pl.semaphore_signal(
-        barrier, inc=1, device_id=group_target(d), device_id_type=pl.DeviceIdType.MESH))
 
     flows = []
     for i, (dx, dy, src, dst) in enumerate((
@@ -141,9 +164,11 @@
         up_s[i] = jnp.where(low8, first, turned)
         down_s[i] = jnp.where(low8, turned, first)
 
-    pl.semaphore_wait(barrier, total - 1)
+    pl.semaphore_wait(barrier, adjacent_count)
     for copy, to_ok, from_ok, dst in flows:
         pl.when(to_ok)(copy.start)
+    if rounds > 0:
+        signal_adjacent(relay.at[0])
 
     for copy, to_ok, from_ok, dst in flows:
         @pl.when(jnp.logical_not(from_ok))
@@ -224,7 +249,10 @@
             pa[m, 1, z + 1] = root * v
         return carry
 
-    lax.fori_loop(0, layers, roots_step, 0)
+    lax.fori_loop(0, layers, roots_step, 0, unroll=2)
+    for k in range(1, rounds):
+        pl.semaphore_wait(relay.at[k - 1], adjacent_count)
+        signal_adjacent(relay.at[k])
 
     def image(m, c, z, field, p_ref):
         across = tr[m, c, z]
@@ -250,7 +278,7 @@
                 carry[m] = carry[m] + core * core
         return tuple(carry)
 
-    rr = lax.fori_loop(0, layers, residual_step, (zero_core,) * members)
+    rr = lax.fori_loop(0, layers, residual_step, (zero_core,) * members, unroll=2)
 
     peer = {"ens": lax.rem(ie + 1, ne)}
 
@@ -276,7 +304,7 @@
                 carry[2 * m + 1] = carry[2 * m + 1] + core * core
         return tuple(carry)
 
-    ra_aa = lax.fori_loop(0, layers, image_step, (zero_core,) * (2 * members))
+    ra_aa = lax.fori_loop(0, layers, image_step, (zero_core,) * (2 * members), unroll=2)
     peer_flows[1].start()
 
     def second_step(z, carry):
@@ -288,7 +316,7 @@
                 carry[m] = carry[m] + a[0, 0:rows] * b[0, 0:rows]
         return tuple(carry)
 
-    ab = lax.fori_loop(0, layers, second_step, (zero_core,) * members)
+    ab = lax.fori_loop(0, layers, second_step, (zero_core,) * members, unroll=2)
     peer_flows[2].start()
 
     lane_1 = iota((1, cols), 1)
@@ -298,6 +326,9 @@
             value = jnp.sum(jnp.sum(acc, axis=0, keepdims=True), axis=1, keepdims=True)
             mine = jnp.where(lane_1 == 4 * m + q, value, mine)
     gram_s[0] = mine
+
+    if rounds > 0:
+        pl.semaphore_wait(relay.at[rounds - 1], adjacent_count)
 
     def gram_copy(d):
         return pltpu.make_async_remote_copy(
@@ -372,10 +403,10 @@
     return pl.pallas_call(
         functools.partial(kernel, sizes),
         out_shape=jax.ShapeDtypeStruct((2, layers, rows, cols), f32),
-        in_specs=[pl.BlockSpec(memory_space=pltpu.SMEM)] + [any_space] * 4,
+        in_specs=[any_space] * 5,
         out_specs=pl.BlockSpec(memory_space=pltpu.VMEM),
         scratch_shapes=[
-            vmem(*core), vmem(levels, rows, cols),
+            pltpu.SMEM((members,), jnp.int32), vmem(*core), vmem(levels, rows, cols),
             pltpu.VMEM((rows, cols), jnp.int32), pltpu.VMEM((rows, cols), jnp.int32),
             vmem(pairs, 8, cols), vmem(pairs, 8, cols), vmem(groups, rows, cols), vmem(groups, 8, cols),
             vmem(pairs, 8, cols), vmem(pairs, 8, cols), vmem(2, groups, rows, cols),
@@ -388,13 +419,14 @@
             vmem(*core), vmem(*core), vmem(*core[1:]),
             vmem(*core), vmem(*core), vmem(*core[1:]),
             vmem(1, 1, cols), vmem(total, 1, cols),
-            pltpu.SemaphoreType.DMA((4,)),
+            pltpu.SemaphoreType.REGULAR((max(sizes[0], sizes[1]),)),
+            pltpu.SemaphoreType.DMA((5,)),
             pltpu.SemaphoreType.DMA((8,)), pltpu.SemaphoreType.DMA((8,)),
             pltpu.SemaphoreType.DMA((3,)), pltpu.SemaphoreType.DMA((3,)),
             pltpu.SemaphoreType.DMA, pltpu.SemaphoreType.DMA,
         ],
         compiler_params=pltpu.CompilerParams(
-            collective_id=0, has_side_effects=True, vmem_limit_bytes=40 * 1024 * 1024),
+            collective_id=0, has_side_effects=True),
         name="picard",
     )(friction_rows, u_prior, friction_table, bed_fixed, ice_mask)
 

time: 26.5 us -> 21.5 us (0.81)
  local copies, waits for them, and re-layouts: 4.59 us -> 1.59 us
  Pallas kernels: 21.6 us -> 19.8 us
    unnamed x11 -> x1, local copies, waits for them, and re-layouts: 4.59 us -> 1.59 us
    pallas_call x1, Pallas kernels: 21.6 us -> 19.8 us  [body(): pl.pallas_call(functools.partial(kernel, sizes), out_shape=jax.ShapeDtype...]
where the time goes in v2:
time: 21.5 us; the launch traced here: 21.4 us
  Pallas kernels  19.8 us (92%)
  local copies, waits for them, and re-layouts  1.59 us (7%)
    pallas_call x1, Pallas kernels, body(): pl.pallas_call(functools.partial(kernel, sizes), out_shape=jax.ShapeDtype...  19.8 us
    unnamed x1, local copies, waits for them, and re-layouts  1.59 us

profile of v2, /device:TPU:0, one launch (start us, length us, event | category | flops | bytes accessed | tf_op | source)
XLA Modules:
  0.0 21.4 jit_solution(15509649452812178954)
XLA Ops:
  0.0 19.8 %picard.1 = f32[2,10,16,128]{3,2,1,0:T(8,128)} custom-call(s32[2]{0:T(128)} %rows_hbm.1, f32[2,2,10,16,128]{4,3,2,1,0:T(8,128)} %u_hbm.1, f32[16,16,128]{2,1,0:T(8,128)} %table_hbm.1, s32[16,128]{1,0:T(8,128)} %bed_hbm.1, s32[16,128]{1,0:T(8,128)} %mask_hbm.1), custom_call_target="tpu_custom_call" | custom-call | tf_op jit(solution)/shard_map/picard/pallas_call | solution.py:403
  19.8 1.6 %copy.7 = f32[2,10,16,128]{3,2,1,0:T(8,128)} copy(f32[2,10,16,128]{3,2,1,0:T(8,128)} %picard.1) | data formatting | bytes 327680

commit v3 on v2

--- a/solution.py
+++ b/solution.py
@@ -36,6 +36,19 @@
 
 def spread_z(ref, index, z):
     return ref[index + (z + 1,)] + 0.5 * (ref[index + (z,)] + ref[index + (z + 2,)])
+
+
+def chunk_places(members, layers):
+    chunks, places, pair, group = [], [], 0, 0
+    for m in range(members):
+        base = 2 + members if m == 0 else 0
+        base_even = base + base % 2
+        count = base_even + 2 * layers
+        pairs, groups = count // 2, (count + SLOTS - 1) // SLOTS
+        chunks.append((pair, pairs, group, groups))
+        places.append(base_even)
+        pair, group = pair + pairs, group + groups
+    return chunks, places
 
 
 def kernel(sizes, rows_hbm, u_hbm, table_hbm, bed_hbm, mask_hbm, out_ref,
@@ -107,7 +120,21 @@
                 return carry
             lax.fori_loop(1, total, step, 0)
 
-    flows = []
+    shared = [
+        lambda: bed_v[...].astype(jnp.float32) * bed_unit,
+        lambda: mask_v[...].astype(jnp.float32),
+    ] + [(lambda m=m: table_v[rows_ref[m]]) for m in range(members)]
+    if len(shared) % 2:
+        shared.append(shared[-1])
+    chunks, places = chunk_places(members, layers)
+    readers = [
+        (shared if m == 0 else [])
+        + [(lambda m=m, c=c, z=z: u_v[m, c, z]) for z in range(layers) for c in range(2)]
+        for m in range(members)
+    ]
+
+    flows = [[] for _ in chunks]
+    absent = []
     for i, (dx, dy, src, dst) in enumerate((
         (-1, 0, up_s, below_r),
         (1, 0, down_s, above_r),
@@ -122,56 +149,48 @@
         sx, sy = ix - dx, iy - dy
         to_ok = (tx >= 0) & (tx < np_) & (ty >= 0) & (ty < nq)
         from_ok = (sx >= 0) & (sx < np_) & (sy >= 0) & (sy < nq)
-        copy = pltpu.make_async_remote_copy(
-            src_ref=src, dst_ref=dst, send_sem=halo_send.at[i], recv_sem=halo_recv.at[i],
-            device_id={"plane": jnp.clip(tx, 0, np_ - 1), "planey": jnp.clip(ty, 0, nq - 1)},
-            device_id_type=pl.DeviceIdType.MESH)
-        flows.append((copy, to_ok, from_ok, dst))
+        absent.append((jnp.logical_not(from_ok), dst))
+        for k, (pair, pairs, group, groups) in enumerate(chunks):
+            part = pl.ds(pair, pairs) if i < 2 else pl.ds(group, groups)
+            copy = pltpu.make_async_remote_copy(
+                src_ref=src.at[part], dst_ref=dst.at[part],
+                send_sem=halo_send.at[8 * k + i], recv_sem=halo_recv.at[8 * k + i],
+                device_id={"plane": jnp.clip(tx, 0, np_ - 1), "planey": jnp.clip(ty, 0, nq - 1)},
+                device_id_type=mesh_id)
+            flows[k].append((copy, to_ok, from_ok))
 
     for load in loads:
         load.wait()
 
-    planes = [(lambda m=m, c=c, z=z: u_v[m, c, z])
-              for m in range(members) for z in range(layers) for c in range(2)]
-    first_extra = len(planes)
-    planes.append(lambda: bed_v[...].astype(jnp.float32) * bed_unit)
-    planes.append(lambda: mask_v[...].astype(jnp.float32))
-    for m in range(members):
-        planes.append(lambda m=m: table_v[rows_ref[m]])
-    if len(planes) % 2:
-        planes.append(planes[-1])
-    groups = side_s.shape[0]
-
     low8 = iota((8, cols), 0) < 4
     lane_x = iota((rows, cols), 1)
-    for g in range(groups):
-        packed = jnp.zeros((rows, cols), jnp.float32)
-        for k in range(SLOTS):
-            p = g * SLOTS + k
-            if p >= len(planes):
-                continue
-            rolled = pltpu.roll(planes[p](), (8 * k + 4) % cols, 1)
-            packed = jnp.where((lane_x // 8) == k, rolled, packed)
-        side_s[g] = packed
-        corner_s[g] = jnp.where(low8, packed[0:8], packed[rows - 8:rows])
 
     def ends(value):
         return jnp.where(low8, value[0:8], value[rows - 8:rows])
 
-    for i in range(len(planes) // 2):
-        first = ends(planes[2 * i]())
-        turned = pltpu.roll(ends(planes[2 * i + 1]()), 4, 0)
-        up_s[i] = jnp.where(low8, first, turned)
-        down_s[i] = jnp.where(low8, turned, first)
+    for (pair, pairs, group, groups), read in zip(chunks, readers):
+        for g in range(groups):
+            packed = jnp.zeros((rows, cols), jnp.float32)
+            for k in range(min(SLOTS, len(read) - g * SLOTS)):
+                rolled = pltpu.roll(read[g * SLOTS + k](), (8 * k + 4) % cols, 1)
+                packed = jnp.where((lane_x // 8) == k, rolled, packed)
+            side_s[group + g] = packed
+            corner_s[group + g] = ends(packed)
+        for i in range(pairs):
+            first = ends(read[2 * i]())
+            turned = pltpu.roll(ends(read[min(2 * i + 1, len(read) - 1)]()), 4, 0)
+            up_s[pair + i] = jnp.where(low8, first, turned)
+            down_s[pair + i] = jnp.where(low8, turned, first)
 
     pl.semaphore_wait(barrier, adjacent_count)
-    for copy, to_ok, from_ok, dst in flows:
-        pl.when(to_ok)(copy.start)
+    for chunk in flows:
+        for copy, to_ok, from_ok in chunk:
+            pl.when(to_ok)(copy.start)
     if rounds > 0:
         signal_adjacent(relay.at[0])
 
-    for copy, to_ok, from_ok, dst in flows:
-        @pl.when(jnp.logical_not(from_ok))
+    for gone, dst in absent:
+        @pl.when(gone)
         def _(dst=dst):
             dst[...] = jnp.zeros(dst.shape, jnp.float32)
     zero = jnp.zeros((2, ring, cols), jnp.float32)
@@ -190,139 +209,138 @@
                 summed = summed + u_v[m, c, z]
             w_core[c, z] = cover_core * summed
 
-    for copy, to_ok, from_ok, dst in flows:
-        pl.when(from_ok)(copy.wait_recv)
-
-    lane_h = iota((rows, cols), 1)
-    lane_8 = iota((8, cols), 1)
-    for g in range(groups):
-        hx[g, 0:rows] = jnp.where(lane_h % 8 < 4, side_r[0, g], side_r[1, g])
-        left = jnp.where(low8, corner_r[0, 0, g], corner_r[1, 0, g])
-        right = jnp.where(low8, corner_r[0, 1, g], corner_r[1, 1, g])
-        hx[g, rows:ring] = jnp.where(lane_8 % 8 < 4, left, right)
-
-    def tail(p):
-        i = p // 2
+    def arrive(k):
+        for copy, to_ok, from_ok in flows[k]:
+            pl.when(from_ok)(copy.wait_recv)
+        _, _, group, groups = chunks[k]
+        for g in range(group, group + groups):
+            hx[g, 0:rows] = jnp.where(lane_x % 8 < 4, side_r[0, g], side_r[1, g])
+            left = jnp.where(low8, corner_r[0, 0, g], corner_r[1, 0, g])
+            right = jnp.where(low8, corner_r[0, 1, g], corner_r[1, 1, g])
+            hx[g, rows:ring] = jnp.where(lane_x[0:8] % 8 < 4, left, right)
+
+    def extended(k, p):
+        pair, _, group, _ = chunks[k]
+        i = pair + p // 2
         if p % 2 == 0:
-            return jnp.where(low8, below_r[i], above_r[i])
-        return pltpu.roll(jnp.where(low8, above_r[i], below_r[i]), 4, 0)
-
-    def extended(p):
-        core = jnp.concatenate([planes[p](), tail(p)], axis=0)
-        k = p % SLOTS
-        halo = pltpu.roll(hx[p // SLOTS], (-(8 * k + 4)) % cols, 1)
+            tail = jnp.where(low8, below_r[i], above_r[i])
+        else:
+            tail = pltpu.roll(jnp.where(low8, above_r[i], below_r[i]), 4, 0)
+        core = jnp.concatenate([readers[k][p](), tail], axis=0)
+        halo = pltpu.roll(hx[group + p // SLOTS], (-(8 * (p % SLOTS) + 4)) % cols, 1)
         return jnp.stack([core, halo])
 
-    p = 0
-    for m in range(members):
+    def assemble(m):
+        arrive(m)
+        base = places[m]
         for z in range(layers):
             for c in range(2):
-                ext[m, c, z + 1] = extended(p)
-                p += 1
-    bed = extended(first_extra)
-    cover = extended(first_extra + 1)
-    row = iota((2, ring, cols), 1)
-    position = (ix * rows + jnp.where(row < rows + HALO, row, row - ring)).astype(jnp.float32)
-    thickness = 1.0 + 2.0 * position / (np_ * rows - 1)
-    slope_x = (shift_i(bed, 1) - shift_i(bed, -1)) * 0.5
-    slope_y = (shift_j(bed, 1) - shift_j(bed, -1)) * 0.5
-    force[0] = -(cover * thickness * slope_x)
-    force[1] = -(cover * thickness * slope_y)
-    force[2] = cover
-    for m in range(members):
-        force[3 + m] = cover * extended(first_extra + 2 + m)
-
-    def roots_step(z, carry):
-        cover = force[2]
-        for m in range(members):
-            u, v = ext[m, 0, z + 1], ext[m, 1, z + 1]
-            u_i = (shift_i(u, 1) - shift_i(u, -1)) * 0.5
-            v_j = (shift_j(v, 1) - shift_j(v, -1)) * 0.5
-            shear = ((shift_j(u, 1) - shift_j(u, -1)) + (shift_i(v, 1) - shift_i(v, -1))) * 0.5
-            u_z = (ext[m, 0, z + 2] - ext[m, 0, z]) * 0.5
-            v_z = (ext[m, 1, z + 2] - ext[m, 1, z]) * 0.5
-            strain = (u_i * u_i + v_j * v_j + u_i * v_j + 0.25 * shear * shear
-                      + 0.25 * (u_z * u_z + v_z * v_z))
-            root = cover * jnp.exp(jnp.log(strain + 0.1) * (-1.0 / 6.0))
-            roots[m, z + 1] = root
-            pa[m, 0, z + 1] = root * u
-            pa[m, 1, z + 1] = root * v
-        return carry
-
-    lax.fori_loop(0, layers, roots_step, 0, unroll=2)
-    for k in range(1, rounds):
-        pl.semaphore_wait(relay.at[k - 1], adjacent_count)
-        signal_adjacent(relay.at[k])
+                ext[m, c, z + 1] = extended(m, base + 2 * z + c)
+        if m > 0:
+            return
+        bed = extended(0, 0)
+        cover = extended(0, 1)
+        row = iota((2, ring, cols), 1)
+        position = (ix * rows + jnp.where(row < rows + HALO, row, row - ring)).astype(jnp.float32)
+        thickness = 1.0 + 2.0 * position / (np_ * rows - 1)
+        slope_x = (shift_i(bed, 1) - shift_i(bed, -1)) * 0.5
+        slope_y = (shift_j(bed, 1) - shift_j(bed, -1)) * 0.5
+        force[0] = -(cover * thickness * slope_x)
+        force[1] = -(cover * thickness * slope_y)
+        force[2] = cover
+        for k in range(members):
+            force[3 + k] = cover * extended(0, 2 + k)
+
+    def roots_step(m, z):
+        u, v = ext[m, 0, z + 1], ext[m, 1, z + 1]
+        u_i = (shift_i(u, 1) - shift_i(u, -1)) * 0.5
+        v_j = (shift_j(v, 1) - shift_j(v, -1)) * 0.5
+        shear = ((shift_j(u, 1) - shift_j(u, -1)) + (shift_i(v, 1) - shift_i(v, -1))) * 0.5
+        u_z = (ext[m, 0, z + 2] - ext[m, 0, z]) * 0.5
+        v_z = (ext[m, 1, z + 2] - ext[m, 1, z]) * 0.5
+        strain = (u_i * u_i + v_j * v_j + u_i * v_j + 0.25 * shear * shear
+                  + 0.25 * (u_z * u_z + v_z * v_z))
+        root = force[2] * jnp.exp(jnp.log(strain + 0.1) * (-1.0 / 6.0))
+        roots[m, z + 1] = root
+        pa[m, 0, z + 1] = root * u
+        pa[m, 1, z + 1] = root * v
 
     def image(m, c, z, field, p_ref):
-        across = tr[m, c, z]
-        bottom = jnp.where(z == 0, 1.0, 0.0).astype(jnp.float32)
-        diag = force[3 + m] * bottom + (1.0 - force[2])
+        diag = 1.0 - force[2]
+        if z == 0:
+            diag = diag + force[3 + m]
         spread = spread_ij(spread_z(p_ref, (m, c), z), c)
-        return 4.0 * roots[m, z + 1] * (across * field - spread) + diag * field
-
-    zero_core = jnp.zeros((rows, cols), jnp.float32)
-
-    def residual_step(z, carry):
-        carry = list(carry)
-        for m in range(members):
-            near = spread_z(roots, (m,), z)
-            for c in range(2):
-                tr[m, c, z] = spread_ij(near, c)
-                start = force[2] * ext[m, c, z + 1]
-                r = force[c] - image(m, c, z, start, pa)
-                r_ext[m, c, z] = r
-                pb[m, c, z + 1] = roots[m, z + 1] * r
-                core = r[0, 0:rows]
-                r_core[m, c, z] = core
-                carry[m] = carry[m] + core * core
-        return tuple(carry)
-
-    rr = lax.fori_loop(0, layers, residual_step, (zero_core,) * members, unroll=2)
+        return 4.0 * roots[m, z + 1] * (tr[m, c, z] * field - spread) + diag * field
+
+    def residual_step(m, z, acc):
+        near = spread_z(roots, (m,), z)
+        for c in range(2):
+            tr[m, c, z] = spread_ij(near, c)
+            r = force[c] - image(m, c, z, force[2] * ext[m, c, z + 1], pa)
+            r_ext[m, c, z] = r
+            pb[m, c, z + 1] = roots[m, z + 1] * r
+            core = r[0, 0:rows]
+            r_core[m, c, z] = core
+            acc = acc + core * core
+        return acc
+
+    def image_step(m, z, ra, aa):
+        for c in range(2):
+            r = r_ext[m, c, z]
+            a = image(m, c, z, r, pb)
+            a_ext[m, c, z] = a
+            pa[m, c, z + 1] = roots[m, z + 1] * a
+            core = a[0, 0:rows]
+            a_core[m, c, z] = core
+            ra = ra + r[0, 0:rows] * core
+            aa = aa + core * core
+        return ra, aa
+
+    def second_step(m, z, ab):
+        for c in range(2):
+            a = a_ext[m, c, z]
+            b = image(m, c, z, a, pa)
+            ab = ab + a[0, 0:rows] * b[0, 0:rows]
+        return ab
 
     peer = {"ens": lax.rem(ie + 1, ne)}
 
     def to_peer(i, src, dst):
         return pltpu.make_async_remote_copy(
             src_ref=src, dst_ref=dst, send_sem=peer_send.at[i], recv_sem=peer_recv.at[i],
-            device_id=peer, device_id_type=pl.DeviceIdType.MESH)
-
-    peer_flows = [to_peer(0, w_core, w_peer), to_peer(1, r_core, r_peer), to_peer(2, a_core, a_peer)]
-    peer_flows[0].start()
-
-    def image_step(z, carry):
-        carry = list(carry)
-        for m in range(members):
-            for c in range(2):
-                r = r_ext[m, c, z]
-                a = image(m, c, z, r, pb)
-                a_ext[m, c, z] = a
-                pa[m, c, z + 1] = roots[m, z + 1] * a
-                core = a[0, 0:rows]
-                a_core[m, c, z] = core
-                carry[2 * m] = carry[2 * m] + r[0, 0:rows] * core
-                carry[2 * m + 1] = carry[2 * m + 1] + core * core
-        return tuple(carry)
-
-    ra_aa = lax.fori_loop(0, layers, image_step, (zero_core,) * (2 * members), unroll=2)
-    peer_flows[1].start()
-
-    def second_step(z, carry):
-        carry = list(carry)
-        for m in range(members):
-            for c in range(2):
-                a = a_ext[m, c, z]
-                b = image(m, c, z, a, pa)
-                carry[m] = carry[m] + a[0, 0:rows] * b[0, 0:rows]
-        return tuple(carry)
-
-    ab = lax.fori_loop(0, layers, second_step, (zero_core,) * members, unroll=2)
-    peer_flows[2].start()
+            device_id=peer, device_id_type=mesh_id)
+
+    peer_flows = [to_peer(0, w_core, w_peer)]
+    for m in range(members):
+        peer_flows.append(to_peer(2 * m + 1, r_core.at[m], r_peer.at[m]))
+        peer_flows.append(to_peer(2 * m + 2, a_core.at[m], a_peer.at[m]))
+
+    zero_core = jnp.zeros((rows, cols), jnp.float32)
+    grams = []
+    for m in range(members):
+        assemble(m)
+        for z in range(layers):
+            roots_step(m, z)
+        if m == 0:
+            peer_flows[0].start()
+            for k in range(1, rounds):
+                pl.semaphore_wait(relay.at[k - 1], adjacent_count)
+                signal_adjacent(relay.at[k])
+        rr = ra = aa = ab = zero_core
+        for z in range(layers):
+            rr = residual_step(m, z, rr)
+        for z in range(layers):
+            ra, aa = image_step(m, z, ra, aa)
+        peer_flows[2 * m + 1].start()
+        for z in range(layers):
+            ab = second_step(m, z, ab)
+        peer_flows[2 * m + 2].start()
+        grams.append((rr, ra, aa, ab))
 
     lane_1 = iota((1, cols), 1)
     mine = jnp.zeros((1, cols), jnp.float32)
     for m in range(members):
-        for q, acc in enumerate((rr[m], ra_aa[2 * m], ra_aa[2 * m + 1], ab[m])):
+        for q, acc in enumerate(grams[m]):
             value = jnp.sum(jnp.sum(acc, axis=0, keepdims=True), axis=1, keepdims=True)
             mine = jnp.where(lane_1 == 4 * m + q, value, mine)
     gram_s[0] = mine
@@ -380,8 +398,9 @@
 
     lax.fori_loop(0, layers, final_step, 0)
 
-    for copy, to_ok, from_ok, dst in flows:
-        pl.when(to_ok)(copy.wait_send)
+    for chunk in flows:
+        for copy, to_ok, from_ok in chunk:
+            pl.when(to_ok)(copy.wait_send)
     for flow in peer_flows:
         flow.wait_send()
     everything.wait_send()
@@ -392,9 +411,9 @@
     levels = friction_table.shape[0]
     total = sizes[0] * sizes[1] * sizes[2]
     ring = rows + 2 * HALO
-    planes = members * layers * 2 + 2 + members
-    pairs = (planes + 1) // 2
-    groups = (2 * pairs + SLOTS - 1) // SLOTS
+    chunks, _ = chunk_places(members, layers)
+    pairs = sum(chunk[1] for chunk in chunks)
+    groups = sum(chunk[3] for chunk in chunks)
     f32 = jnp.float32
     any_space = pl.BlockSpec(memory_space=pl.ANY)
     vmem = lambda *shape: pltpu.VMEM(shape, f32)
@@ -421,8 +440,8 @@
             vmem(1, 1, cols), vmem(total, 1, cols),
             pltpu.SemaphoreType.REGULAR((max(sizes[0], sizes[1]),)),
             pltpu.SemaphoreType.DMA((5,)),
-            pltpu.SemaphoreType.DMA((8,)), pltpu.SemaphoreType.DMA((8,)),
-            pltpu.SemaphoreType.DMA((3,)), pltpu.SemaphoreType.DMA((3,)),
+            pltpu.SemaphoreType.DMA((8 * members,)), pltpu.SemaphoreType.DMA((8 * members,)),
+            pltpu.SemaphoreType.DMA((2 * members + 1,)), pltpu.SemaphoreType.DMA((2 * members + 1,)),
             pltpu.SemaphoreType.DMA, pltpu.SemaphoreType.DMA,
         ],
         compiler_params=pltpu.CompilerParams(

time: 21.5 us -> 20.1 us (0.935)
  Pallas kernels: 19.8 us -> 18.3 us
    pallas_call x1, Pallas kernels: 19.8 us -> 18.3 us  [body(): pl.pallas_call(functools.partial(kernel, sizes), out_shape=jax.ShapeDtype...]
where the time goes in v3:
time: 20.1 us; the launch traced here: 19.9 us
  Pallas kernels  18.3 us (91%)
  local copies, waits for them, and re-layouts  1.59 us (8%)
    pallas_call x1, Pallas kernels, body(): pl.pallas_call(functools.partial(kernel, sizes), out_shape=jax.ShapeDtype...  18.3 us
    unnamed x1, local copies, waits for them, and re-layouts  1.59 us

profile of v3, /device:TPU:0, one launch (start us, length us, event | category | flops | bytes accessed | tf_op | source)
XLA Modules:
  0.0 19.9 jit_solution(16182443773679428014)
XLA Ops:
  0.0 18.3 %picard.1 = f32[2,10,16,128]{3,2,1,0:T(8,128)} custom-call(s32[2]{0:T(128)} %rows_hbm.1, f32[2,2,10,16,128]{4,3,2,1,0:T(8,128)} %u_hbm.1, f32[16,16,128]{2,1,0:T(8,128)} %table_hbm.1, s32[16,128]{1,0:T(8,128)} %bed_hbm.1, s32[16,128]{1,0:T(8,128)} %mask_hbm.1), custom_call_target="tpu_custom_call" | custom-call | tf_op jit(solution)/shard_map/picard/pallas_call | solution.py:422
  18.3 1.6 %copy.7 = f32[2,10,16,128]{3,2,1,0:T(8,128)} copy(f32[2,10,16,128]{3,2,1,0:T(8,128)} %picard.1) | data formatting | bytes 327680

commit v4 on v3

--- a/solution.py
+++ b/solution.py
@@ -248,6 +248,7 @@
         force[0] = -(cover * thickness * slope_x)
         force[1] = -(cover * thickness * slope_y)
         force[2] = cover
+        force[3 + members] = 2.0 * cover
         for k in range(members):
             force[3 + k] = cover * extended(0, 2 + k)
 
@@ -260,22 +261,22 @@
         v_z = (ext[m, 1, z + 2] - ext[m, 1, z]) * 0.5
         strain = (u_i * u_i + v_j * v_j + u_i * v_j + 0.25 * shear * shear
                   + 0.25 * (u_z * u_z + v_z * v_z))
-        root = force[2] * jnp.exp(jnp.log(strain + 0.1) * (-1.0 / 6.0))
+        root = force[3 + members] * jnp.exp(jnp.log(strain + 0.1) * (-1.0 / 6.0))
         roots[m, z + 1] = root
         pa[m, 0, z + 1] = root * u
         pa[m, 1, z + 1] = root * v
 
     def image(m, c, z, field, p_ref):
+        spread = spread_ij(spread_z(p_ref, (m, c), z), c)
+        return tr[m, c, z] * field - roots[m, z + 1] * spread
+
+    def residual_step(m, z, acc):
+        near = spread_z(roots, (m,), z)
         diag = 1.0 - force[2]
         if z == 0:
             diag = diag + force[3 + m]
-        spread = spread_ij(spread_z(p_ref, (m, c), z), c)
-        return 4.0 * roots[m, z + 1] * (tr[m, c, z] * field - spread) + diag * field
-
-    def residual_step(m, z, acc):
-        near = spread_z(roots, (m,), z)
         for c in range(2):
-            tr[m, c, z] = spread_ij(near, c)
+            tr[m, c, z] = roots[m, z + 1] * spread_ij(near, c) + diag
             r = force[c] - image(m, c, z, force[2] * ext[m, c, z + 1], pa)
             r_ext[m, c, z] = r
             pb[m, c, z + 1] = roots[m, z + 1] * r
@@ -434,7 +435,7 @@
             vmem(members, 2, layers, *wide),
             vmem(members, 2, layers + 2, *wide), vmem(members, 2, layers + 2, *wide),
             vmem(members, 2, layers, *wide), vmem(members, 2, layers, *wide),
-            vmem(3 + members, *wide),
+            vmem(4 + members, *wide),
             vmem(*core), vmem(*core), vmem(*core[1:]),
             vmem(*core), vmem(*core), vmem(*core[1:]),
             vmem(1, 1, cols), vmem(total, 1, cols),

time: 20.1 us -> 20 us (level)
  no operation moved by 1% of the time
where the time goes in v4:
time: 20 us; the launch traced here: 19.9 us
  Pallas kernels  18.2 us (91%)
  local copies, waits for them, and re-layouts  1.59 us (8%)
    pallas_call x1, Pallas kernels, body(): pl.pallas_call(functools.partial(kernel, sizes), out_shape=jax.ShapeDtype...  18.2 us
    unnamed x1, local copies, waits for them, and re-layouts  1.59 us

profile of v4, /device:TPU:0, one launch (start us, length us, event | category | flops | bytes accessed | tf_op | source)
XLA Modules:
  0.0 19.9 jit_solution(15344026692700223578)
XLA Ops:
  0.0 18.2 %picard.1 = f32[2,10,16,128]{3,2,1,0:T(8,128)} custom-call(s32[2]{0:T(128)} %rows_hbm.1, f32[2,2,10,16,128]{4,3,2,1,0:T(8,128)} %u_hbm.1, f32[16,16,128]{2,1,0:T(8,128)} %table_hbm.1, s32[16,128]{1,0:T(8,128)} %bed_hbm.1, s32[16,128]{1,0:T(8,128)} %mask_hbm.1), custom_call_target="tpu_custom_call" | custom-call | tf_op jit(solution)/shard_map/picard/pallas_call | solution.py:423
  18.3 1.6 %copy.7 = f32[2,10,16,128]{3,2,1,0:T(8,128)} copy(f32[2,10,16,128]{3,2,1,0:T(8,128)} %picard.1) | data formatting | bytes 327680
